TPU v7x, 32 devices: a whole 2x2x4 slice. The times are simulated.
32 devices in a mesh: ctx: 8 (over z, y), head: 4 (over x, core).
Axes of the slice: x: 2, y: 2, z: 4, core: 2. Of those that a mesh axis runs over, the one named last changes fastest.
Arguments:
- queries: bfloat16 [8192, 16, 128], P('ctx', 'head'), may hold values from -240 to 240, as said below
- lookup_arrays: bfloat16 [8192, 4, 128], P('ctx', 'head'), may hold values from -6 to 6
- content_arrays: bfloat16 [8192, 4, 128], P('ctx', 'head'), may hold values from -6 to 6
- selection: int32 [16, 4, 6], P('ctx', 'head'), may hold values from 0 to 15, as said below
- final_mapping: bfloat16 [2048, 4096], P('head'), may hold values from -0.125 to 0.125
Outputs:
- layer_out: bfloat16 [8192, 4096], P(('ctx', 'head'))
Inputs may be any that keep to these rules, and one draw needn't show every extreme that they name: `queries`: entries lie within -240 and 240. selection[b, h, :] holds 6 block numbers no larger than b; those smaller than b are distinct, and an entry equal to b names nothing. For each KV head and each index c of ctx, the selections of the 2 blocks held at c name, among the blocks held at any one index below c, at most one distinct block, and this bound is met.
All inputs are finite; a program needn't handle non-finite values.
Results may differ from a plain program's by a relative error of at most 0.01.
Values may be sent and summed in bfloat16 or wider, within the bound.
A program may use at most 128 MiB of HBM per device.

v0:
```python
import jax
import jax.numpy as jnp
from jax import lax
from jax.sharding import PartitionSpec as P


def attend_block(operands):
    query_block, key_block, value_block, permitted_mask = operands
    block_size = query_block.shape[0]
    scaling = query_block.shape[-1] ** (-0.5)
    affinity_grid = (
        jnp.einsum("qgd,skd->gqsk", query_block, key_block, preferred_element_type=jnp.float32)
        * scaling
    )
    causal = jnp.arange(block_size)[:, None] >= jnp.arange(block_size)[None, :]
    slot_count = key_block.shape[0]
    own_slot = jnp.arange(slot_count) == slot_count - 1
    allowed = permitted_mask[:, None, None] & (~own_slot[:, None, None] | causal[None])
    allowed = allowed.transpose(1, 0, 2)[None]
    affinity_grid = jnp.where(allowed, affinity_grid, -jnp.inf)
    row_peak = jnp.max(affinity_grid, axis=(2, 3), keepdims=True)
    weights = jnp.exp(affinity_grid - row_peak)
    totals = jnp.sum(weights, axis=(2, 3))
    mixed_result = jnp.einsum(
        "gqsk,skd->qgd",
        weights.astype(jnp.bfloat16),
        value_block,
        preferred_element_type=jnp.float32,
    )
    return (mixed_result / totals.T[:, :, None]).astype(jnp.bfloat16)


def body(queries, lookup_arrays, content_arrays, selection, final_mapping):
    ctx_count = lax.axis_size("ctx")
    position = lax.axis_index("ctx")
    blocks_here = selection.shape[0]
    tokens_here = queries.shape[0]
    block_size = tokens_here // blocks_here
    askers_per_leader = queries.shape[1]
    head_dim = queries.shape[2]
    stacked = jnp.stack(
        [
            lookup_arrays.reshape(blocks_here, block_size, head_dim),
            content_arrays.reshape(blocks_here, block_size, head_dim),
        ]
    )
    chosen = selection[:, 0, :]
    holder_list = chosen // blocks_here
    distant = holder_list <= position - 1
    peer_ids = jnp.arange(ctx_count, dtype=jnp.int32)
    last_id = ctx_count * blocks_here - 1
    matches = distant[:, :, None] & (holder_list[:, :, None] == peer_ids[None, None, :])
    wanted_ids = jnp.max(jnp.where(matches, chosen[:, :, None], -1), axis=(0, 1))
    coded = jnp.where(wanted_ids >= 0, last_id - wanted_ids, -1).astype(jnp.int32)
    received = lax.all_to_all(
        coded.reshape(ctx_count, 1), "ctx", split_axis=0, concat_axis=0, tiled=True
    ).reshape(ctx_count)
    requested = last_id - received
    local_index = jnp.clip(requested - position * blocks_here, 0, blocks_here - 1)
    packed = jnp.take(stacked, local_index, axis=1)
    arrived = lax.all_to_all(packed, "ctx", split_axis=1, concat_axis=1, tiled=True)
    block_pool = jnp.concatenate([stacked, arrived], axis=1)
    block_ids = position * blocks_here + jnp.arange(blocks_here, dtype=jnp.int32)
    slot_ids = jnp.concatenate([chosen, block_ids[:, None]], axis=1)
    permitted_mask = jnp.concatenate(
        [chosen != block_ids[:, None], jnp.ones((blocks_here, 1), jnp.bool_)], axis=1
    )
    slot_owner = slot_ids // blocks_here
    pool_index = jnp.where(
        slot_owner == position, slot_ids - position * blocks_here, blocks_here + slot_owner
    )
    selected = jnp.take(block_pool, pool_index, axis=1)
    asking_lines = queries.reshape(blocks_here, block_size, askers_per_leader, head_dim)
    mixed_result = lax.map(attend_block, (asking_lines, selected[0], selected[1], permitted_mask))
    flat_rows = mixed_result.reshape(tokens_here, askers_per_leader * head_dim)

    def project():
        part_rows = lax.slice_in_dim(
            flat_rows, 0, lax.axis_size("head") * (tokens_here // lax.axis_size("head")), axis=0
        )
        return jnp.dot(part_rows, final_mapping, preferred_element_type=jnp.float32)

    summed = lax.psum_scatter(
        project().astype(jnp.bfloat16), "head", scatter_dimension=0, tiled=True
    ).astype(jnp.float32)
    return summed.astype(jnp.bfloat16)


def solution(mesh):
    in_specs = (
        P("ctx", "head", None),
        P("ctx", "head", None),
        P("ctx", "head", None),
        P("ctx", "head", None),
        P("head", None),
    )
    out_specs = P(("ctx", "head"), None)
    return jax.shard_map(body, mesh=mesh, in_specs=in_specs, out_specs=out_specs, check_vma=False)
```

profile of v0, /device:TPU:0, one launch (start us, length us, event | category | flops | bytes accessed | tf_op | source)
XLA Modules:
  0.0 254.1 jit_solution(15843986675841685980)
XLA Ops:
  6.5 0.8 copy.48
  7.3 0.8 broadcast_compare_fusion.1
  8.1 0.1 copy.47
  8.1 0.1 copy.46
  8.3 0.1 fusion.26
  8.4 0.7 copy.49
  9.0 7.3 %all-to-all-start = ((s32[8,1,1]{2,1,0:T(1,128)}), s32[8,1,1]{2,1,0:T(1,128)S(1)}, u32[]{:S(2)}, u32[]{:S(2)}) async-start(s32[8,1,1]{2,1,0:T(1,128)} %copy.49), calls=%async_computation | async-start | bytes 8192 | tf_op jit(solution)/shard_map/all_to_all | solution.py:55
  16.4 1.1 pad_maximum_fusion.1
  17.5 5.3 %all-to-all-done = s32[8,1,1]{2,1,0:T(1,128)S(1)} async-done(((s32[8,1,1]{2,1,0:T(1,128)}), s32[8,1,1]{2,1,0:T(1,128)S(1)}, u32[]{:S(2)}, u32[]{:S(2)}) %all-to-all-start) | async-done | bytes 64 | tf_op jit(solution)/shard_map/all_to_all | solution.py:55
  22.8 0.2 clamp_reduce_fusion
  23.0 1.0 gather_fusion
  24.0 0.0 copy-start.4
  24.0 0.0 copy-start.2
  24.0 0.0 copy-start.3
  24.0 1.6 select_bitcast_fusion
  25.6 3.6 %all-to-all-start.1 = ((bf16[2,8,512,128]{3,2,0,1:T(8,128)(2,1)}), bf16[2,8,512,128]{3,2,0,1:T(8,128)(2,1)S(1)}, u32[]{:S(2)}, u32[]{:S(2)}) async-start(bf16[2,8,512,128]{3,2,0,1:T(8,128)(2,1)} %select_bitcast_fusion), calls=%async_computation.1 | async-start | bytes 4194304 | tf_op jit(solution)/shard_map/all_to_all | solution.py:61
  29.2 0.0 reduce-scatter.2.cloned.1.call-start
  29.3 0.0 copy-done.4
  29.3 0.1 compare_select_fusion
  29.4 0.1 reshape.329
  29.5 0.1 compare_and_fusion.1
  29.6 46.6 %all-to-all-done.1 = bf16[2,8,512,128]{3,2,0,1:T(8,128)(2,1)S(1)} async-done(((bf16[2,8,512,128]{3,2,0,1:T(8,128)(2,1)}), bf16[2,8,512,128]{3,2,0,1:T(8,128)(2,1)S(1)}, u32[]{:S(2)}, u32[]{:S(2)}) %all-to-all-start.1) | async-done | bytes 2097184 | tf_op jit(solution)/shard_map/all_to_all | solution.py:61
  76.2 0.2 pad_maximum_fusion
  76.5 0.2 copy.52
  76.7 2.9 %gather_fusion.1 = bf16[14,2,512,128]{3,2,1,0:T(8,128)(2,1)} fusion(bf16[2,10,512,128]{3,2,1,0:T(8,128)(2,1)S(1)} %copy.52, s32[1024]{0:T(1024)S(1)} %pad_clamp_fusion), kind=kCustom, calls=%fused_computation.1 | custom fusion | bytes 7340088 | tf_op jit(solution)/shard_map/jit(_take)/gather | solution.py:72
  79.6 2.4 fusion.23
  82.0 0.0 copy-start
  82.0 2.3 slice_bitcast_fusion
  84.3 83.4 %while.10 = (s32[]{:T(128)}, bf16[2,512,4,128]{3,2,1,0:T(4,128)(2,1)S(1)}, bf16[2,7,512,128]{3,2,1,0:T(8,128)(2,1)}, pred[2,7]{1,0:T(4,128)(4,1)S(1)}, bf16[2,7,...) while((s32[]{:T(128)}, bf16[2,512,4,128]{3,2,1,0:T(4,128)(2,1)S(1)}, ...), condition=%wide.region_4.5_spmd, body=%wide.region_1.4_spmd.sunk | while | flops 3843289088 | bytes 109355664 | solution.py:74
  84.3 0.1 iota_compare_fusion.2
  84.4 1.1 or_and_fusion.2
  85.5 0.2 constant_dynamic-slice_fusion.2
  85.7 13.3 %fusion.38 = (f32[4,512]{1,0:T(4,128)S(1)}, f32[7,512,512,4]{2,1,3,0:T(8,128)}) fusion(pred[512,7,512]{0,2,1:T(8,128)(4,1)S(1)} %or_and_fusion.2, bf16[1,512,4,128]{3,2,1,0:T(4,128)(2,1)S(1)} %constant_dynamic-slice_fusion.2, bf16[2,7,512,128]{3,2,1,0:T(8,128)(2,1)} %get-tuple-element.146, s32[]{:T(128)} %get-tuple-element.135), kind=kOutput, calls=%fused_computation.6.clone.1 | convolution fusion | flops 1901066240 | bytes 32645632 | tf_op jit(solution)/shard_map/while/body/eval_jaxpr/qgd,skd->gqsk/dot_general | solution.py:12
  99.0 12.9 %fusion.39 = f32[4,512]{1,0:T(4,128)S(1)} fusion(f32[7,512,512,4]{2,1,3,0:T(8,128)} %get-tuple-element.126, f32[4,512]{1,0:T(4,128)S(1)} %get-tuple-element.127, pred[512,7,512]{0,2,1:T(8,128)(4,1)S(1)} %or_and_fusion.2), kind=kLoop, calls=%fused_computation.4.clone.1 | loop fusion | flops 29358080 | bytes 31211520 | tf_op jit(solution)/shard_map/while/body/eval_jaxpr/reduce_sum | solution.py:23
  111.9 13.5 %fusion.40 = bf16[1,512,4,128]{1,3,2,0:T(8,128)(2,1)S(1)} fusion(f32[7,512,512,4]{2,1,3,0:T(8,128)} %get-tuple-element.126, f32[4,512]{1,0:T(4,128)S(1)} %get-tuple-element.127, pred[512,7,512]{0,2,1:T(8,128)(4,1)S(1)} %or_and_fusion.2, bf16[2,7,512,128]{3,2,1,0:T(8,128)(2,1)S(1)} %copy-done.1, s32[]{:T(128)} %get-tuple-element.135, ...), kind=kOutput, calls=%fused_computation.13.clone.1 | convolution fusion | flops 1908932608 | bytes 32653316 | tf_op jit(solution)/shard_map/while/body/eval_jaxpr/gqsk,skd->qgd/dot_general | solution.py:24
  125.5 0.3 copy.83
  125.8 0.2 constant_dynamic-update-slice_fusion.2
  126.0 0.1 iota_compare_fusion.2
  126.2 1.1 or_and_fusion.2
  127.2 0.2 constant_dynamic-slice_fusion.2
  127.4 13.3 %fusion.38 = (f32[4,512]{1,0:T(4,128)S(1)}, f32[7,512,512,4]{2,1,3,0:T(8,128)}) fusion(pred[512,7,512]{0,2,1:T(8,128)(4,1)S(1)} %or_and_fusion.2, bf16[1,512,4,128]{3,2,1,0:T(4,128)(2,1)S(1)} %constant_dynamic-slice_fusion.2, bf16[2,7,512,128]{3,2,1,0:T(8,128)(2,1)} %get-tuple-element.146, s32[]{:T(128)} %get-tuple-element.135), kind=kOutput, calls=%fused_computation.6.clone.1 | convolution fusion | flops 1901066240 | bytes 32645632 | tf_op jit(solution)/shard_map/while/body/eval_jaxpr/qgd,skd->gqsk/dot_general | solution.py:12
  140.8 12.9 %fusion.39 = f32[4,512]{1,0:T(4,128)S(1)} fusion(f32[7,512,512,4]{2,1,3,0:T(8,128)} %get-tuple-element.126, f32[4,512]{1,0:T(4,128)S(1)} %get-tuple-element.127, pred[512,7,512]{0,2,1:T(8,128)(4,1)S(1)} %or_and_fusion.2), kind=kLoop, calls=%fused_computation.4.clone.1 | loop fusion | flops 29358080 | bytes 31211520 | tf_op jit(solution)/shard_map/while/body/eval_jaxpr/reduce_sum | solution.py:23
  153.7 13.5 %fusion.40 = bf16[1,512,4,128]{1,3,2,0:T(8,128)(2,1)S(1)} fusion(f32[7,512,512,4]{2,1,3,0:T(8,128)} %get-tuple-element.126, f32[4,512]{1,0:T(4,128)S(1)} %get-tuple-element.127, pred[512,7,512]{0,2,1:T(8,128)(4,1)S(1)} %or_and_fusion.2, bf16[2,7,512,128]{3,2,1,0:T(8,128)(2,1)S(1)} %copy-done.1, s32[]{:T(128)} %get-tuple-element.135, ...), kind=kOutput, calls=%fused_computation.13.clone.1 | convolution fusion | flops 1908932608 | bytes 32653316 | tf_op jit(solution)/shard_map/while/body/eval_jaxpr/gqsk,skd->qgd/dot_general | solution.py:24
  167.2 0.3 copy.83
  167.5 0.2 constant_dynamic-update-slice_fusion.2
  167.8 8.9 %convolution_convert_fusion = bf16[1024,4096]{1,0:T(8,128)(2,1)} fusion(bf16[512,4096]{1,0:T(8,128)(2,1)} %param.11, bf16[128,8,4,128]{3,2,1,0:T(4,128)(2,1)S(1)} %bitcast.113), kind=kOutput, calls=%fused_computation.28 | convolution fusion | flops 4299161600 | bytes 13631488 | tf_op jit(solution)/shard_map/dot_general | solution.py:81
  176.7 0.0 reduce-scatter.2.cloned.1.call-update
  176.7 70.6 %reduce-scatter.2.cloned.1.call-done = bf16[256,4096]{1,0:T(8,128)(2,1)} async-done(((bf16[1024,4096]{1,0:T(8,128)(2,1)}), bf16[256,4096]{1,0:T(8,128)(2,1)}) %reduce-scatter.2.cloned.1.call-update) | async-done | bytes 2097168 | tf_op jit(solution)/shard_map/reduce_scatter | solution.py:83
  (24 shorter events, 0.1 us)
Async XLA Ops:
  9.0 13.7 %all-to-all-start = ((s32[8,1,1]{2,1,0:T(1,128)}), s32[8,1,1]{2,1,0:T(1,128)S(1)}, u32[]{:S(2)}, u32[]{:S(2)}) async-start(s32[8,1,1]{2,1,0:T(1,128)} %copy.49), calls=%async_computation | async-start | bytes 8192 | tf_op jit(solution)/shard_map/all_to_all | solution.py:55
  24.0 5.3 %copy-start.4 = (s32[2,1,6]{2,1,0:T(1,128)S(1)}, s32[2,1,6]{2,1,0:T(1,128)}, u32[]{:S(2)}) copy-start(s32[2,1,6]{2,1,0:T(1,128)} %param.10) | copy-start | bytes 148
  24.0 52.2 %copy-start.2 = (bf16[1024,1,128]{2,0,1:T(8,128)(2,1)S(1)}, bf16[1024,1,128]{2,0,1:T(8,128)(2,1)}, u32[]{:S(2)}) copy-start(bf16[1024,1,128]{2,0,1:T(8,128)(2,1)} %param.9) | copy-start | bytes 786436
  24.0 52.2 %copy-start.3 = (bf16[1024,1,128]{2,0,1:T(8,128)(2,1)S(1)}, bf16[1024,1,128]{2,0,1:T(8,128)(2,1)}, u32[]{:S(2)}) copy-start(bf16[1024,1,128]{2,0,1:T(8,128)(2,1)} %param.8) | copy-start | bytes 786436
  25.6 50.6 %all-to-all-start.1 = ((bf16[2,8,512,128]{3,2,0,1:T(8,128)(2,1)}), bf16[2,8,512,128]{3,2,0,1:T(8,128)(2,1)S(1)}, u32[]{:S(2)}, u32[]{:S(2)}) async-start(bf16[2,8,512,128]{3,2,0,1:T(8,128)(2,1)} %select_bitcast_fusion), calls=%async_computation.1 | async-start | bytes 4194304 | tf_op jit(solution)/shard_map/all_to_all | solution.py:61
  29.2 218.1 %reduce-scatter.2.cloned.1.call-start = ((), (), s32[]{:S(2)}) async-start(), calls=%async_computation.3 | async-start | bytes 10485760 | tf_op jit(solution)/shard_map/reduce_scatter | solution.py:83
  82.0 2.3 copy-start
  82.0 2.3 copy-start.5
  99.0 12.9 %copy-start.1 = (bf16[2,7,512,128]{3,2,1,0:T(8,128)(2,1)S(1)}, bf16[2,7,512,128]{3,2,1,0:T(8,128)(2,1)}, u32[]{:S(2)}) copy-start(bf16[2,7,512,128]{3,2,1,0:T(8,128)(2,1)} %get-tuple-element.144) | copy-start | bytes 5505028 | tf_op jit(solution)/shard_map/while
  140.8 12.9 %copy-start.1 = (bf16[2,7,512,128]{3,2,1,0:T(8,128)(2,1)S(1)}, bf16[2,7,512,128]{3,2,1,0:T(8,128)(2,1)}, u32[]{:S(2)}) copy-start(bf16[2,7,512,128]{3,2,1,0:T(8,128)(2,1)} %get-tuple-element.144) | copy-start | bytes 5505028 | tf_op jit(solution)/shard_map/while
Sparse Core Ops, SparseCore 0:
  176.8 70.4 reduce-scatter.1
where the time goes:
time: 255 us; the launch traced here: 254 us
  waiting for transfers between devices  123 us (48%)
  matrix products  62.6 us (25%)
  other arithmetic  34.7 us (14%)
  between operations  13.6 us (5%)
  starting transfers between devices  11 us (4%)
  local copies, waits for them, and re-layouts  9.59 us (4%)
    reduce_scatter x1, waiting for transfers between devices, body(): lax.psum_scatter(project().astype(jnp.bfloat16), 'head', scatter_dimensio...  70.6 us
    all_to_all x1, waiting for transfers between devices, body(): lax.all_to_all(packed, 'ctx', split_axis=1, concat_axis=1, tiled=True)  46.6 us
    dot_general x2, matrix products, attend_block(): jnp.einsum('gqsk,skd->qgd', weights.astype(jnp.bfloat16), value_block, pr...  27.1 us
    dot_general x2, matrix products, attend_block(): jnp.einsum('qgd,skd->gqsk', query_block, key_block, preferred_element_typ...  26.6 us
    reduce_sum x2, other arithmetic, attend_block(): totals = jnp.sum(weights, axis=(2, 3))  25.8 us
    dot_general x1, matrix products, project(): return jnp.dot(part_rows, final_mapping, preferred_element_type=jnp.float32)  8.92 us
    all_to_all x1, starting transfers between devices, body(): lax.all_to_all(coded.reshape(ctx_count, 1), 'ctx', split_axis=0, concat_a...  7.31 us
    all_to_all x1, waiting for transfers between devices, body(): lax.all_to_all(coded.reshape(ctx_count, 1), 'ctx', split_axis=0, concat_a...  5.29 us
  transfers between devices with their start and end apart: 3, of which 3 were waited for; matrix products, arithmetic and copies ran while one was open for 1% of the time, Pallas kernels for 0%

commit v1 on v0

--- a/solution.py
+++ b/solution.py
@@ -1,7 +1,32 @@
+import functools
 import jax
 import jax.numpy as jnp
 from jax import lax
 from jax.sharding import PartitionSpec as P
+from jax.lax import axis_index, axis_size, ppermute
+
+
+def lift_the_types(vector, out_dim, k_dim):
+    kept_arr = axis_size("ctx")
+    b_now = axis_index("ctx")
+    z_new, s_next = (kept_arr, b_now)
+    y = vector.shape[out_dim] // z_new
+    formed = list(vector.shape)
+    formed[out_dim] = y
+    small = formed[k_dim]
+    formed[k_dim] = small * z_new
+    wide_out = jnp.zeros(formed, vector.dtype)
+    for t in range(z_new):
+        earlier = lax.dynamic_slice_in_dim(vector, (s_next ^ t) * y, y, axis=out_dim)
+        if t:
+            earlier = ppermute(earlier, "ctx", [(pp, pp ^ t) for pp in range(z_new)])
+        wide_out = lax.dynamic_update_slice_in_dim(
+            wide_out, earlier, (s_next ^ t) * small, axis=k_dim
+        )
+    return wide_out
+
+
+show_the_row = functools.partial(lift_the_types, out_dim=1, k_dim=1)
 
 
 def attend_block(operands):
@@ -58,7 +83,7 @@
     requested = last_id - received
     local_index = jnp.clip(requested - position * blocks_here, 0, blocks_here - 1)
     packed = jnp.take(stacked, local_index, axis=1)
-    arrived = lax.all_to_all(packed, "ctx", split_axis=1, concat_axis=1, tiled=True)
+    arrived = show_the_row(packed)
     block_pool = jnp.concatenate([stacked, arrived], axis=1)
     block_ids = position * blocks_here + jnp.arange(blocks_here, dtype=jnp.int32)
     slot_ids = jnp.concatenate([chosen, block_ids[:, None]], axis=1)

time: 255 us -> 255 us (level)
  waiting for transfers between devices: 123 us -> 113 us
  starting transfers between devices: 11 us -> 17.3 us
  local copies, waits for them, and re-layouts: 9.59 us -> 12.2 us
    all_to_all x1 -> x0, waiting for transfers between devices: 46.6 us -> none  [body(): lax.all_to_all(packed, 'ctx', split_axis=1, concat_axis=1, tiled=True)]
    ppermute x0 -> x7, waiting for transfers between devices: none -> 31.3 us  [lift_the_types(): earlier = ppermute(earlier, 'ctx', [(pp, pp ^ t) for pp in range(z_new)])]
    ppermute x0 -> x7, starting transfers between devices: none -> 9.95 us  [lift_the_types(): earlier = ppermute(earlier, 'ctx', [(pp, pp ^ t) for pp in range(z_new)])]
    reduce_scatter x1, waiting for transfers between devices: 70.6 us -> 77.5 us  [body(): lax.psum_scatter(project().astype(jnp.bfloat16), 'head', scatter_dimensio...]
    all_to_all x1 -> x0, starting transfers between devices: 3.6 us -> none  [body(): lax.all_to_all(packed, 'ctx', split_axis=1, concat_axis=1, tiled=True)]
  transfers between devices with their start and end apart: 3 -> 9, of which waited for: 3 -> 6; matrix products, arithmetic and copies ran while one was open for 1% -> 1% of each run, Pallas kernels for 0% -> 0%
where the time goes in v1:
time: 255 us
  waiting for transfers between devices  113 us (44%)
  matrix products  62.6 us (25%)
  other arithmetic  35.7 us (14%)
  starting transfers between devices  17.3 us (7%)
  between operations  13.7 us (5%)
  local copies, waits for them, and re-layouts  12.2 us (5%)
    reduce_scatter x1, waiting for transfers between devices, body(): lax.psum_scatter(project().astype(jnp.bfloat16), 'head', scatter_dimensio...  77.5 us
    ppermute x7, waiting for transfers between devices, lift_the_types(): earlier = ppermute(earlier, 'ctx', [(pp, pp ^ t) for pp in range(z_new)])  31.3 us
    dot_general x2, matrix products, attend_block(): jnp.einsum('gqsk,skd->qgd', weights.astype(jnp.bfloat16), value_block, pr...  27.1 us
    dot_general x2, matrix products, attend_block(): jnp.einsum('qgd,skd->gqsk', query_block, key_block, preferred_element_typ...  26.6 us
    reduce_sum x2, other arithmetic, attend_block(): totals = jnp.sum(weights, axis=(2, 3))  25.8 us
    ppermute x7, starting transfers between devices, lift_the_types(): earlier = ppermute(earlier, 'ctx', [(pp, pp ^ t) for pp in range(z_new)])  9.95 us
    dot_general x1, matrix products, project(): return jnp.dot(part_rows, final_mapping, preferred_element_type=jnp.float32)  8.93 us
    all_to_all x1, starting transfers between devices, body(): lax.all_to_all(coded.reshape(ctx_count, 1), 'ctx', split_axis=0, concat_a...  7.31 us
  transfers between devices with their start and end apart: 9, of which 6 were waited for; matrix products, arithmetic and copies ran while one was open for 1% of the time, Pallas kernels for 0%

profile of v1, /device:TPU:0, one launch (start us, length us, event | category | flops | bytes accessed | tf_op | source)
XLA Modules:
  0.0 254.9 jit_solution(13272840623716062041)
XLA Ops:
  6.5 0.8 copy.35
  7.3 0.8 broadcast_compare_fusion.1
  8.1 0.1 copy.34
  8.1 0.1 copy.33
  8.3 0.1 fusion.26
  8.4 0.7 copy.36
  9.0 7.3 %all-to-all-start = ((s32[8,1,1]{2,1,0:T(1,128)}), s32[8,1,1]{2,1,0:T(1,128)S(1)}, u32[]{:S(2)}, u32[]{:S(2)}) async-start(s32[8,1,1]{2,1,0:T(1,128)} %copy.36), calls=%async_computation | async-start | bytes 8192 | tf_op jit(solution)/shard_map/all_to_all | solution.py:80
  16.4 0.8 compare_select_fusion
  17.3 1.1 pad_maximum_fusion.1
  18.4 4.4 %all-to-all-done = s32[8,1,1]{2,1,0:T(1,128)S(1)} async-done(((s32[8,1,1]{2,1,0:T(1,128)}), s32[8,1,1]{2,1,0:T(1,128)S(1)}, u32[]{:S(2)}, u32[]{:S(2)}) %all-to-all-start) | async-done | bytes 64 | tf_op jit(solution)/shard_map/all_to_all | solution.py:80
  22.8 0.2 clamp_reduce_fusion
  23.0 2.1 gather_fusion
  25.2 1.9 broadcast_select_fusion
  27.1 1.0 dynamic-slice_bitcast_fusion.1
  28.1 0.6 collective-permute-start
  28.6 0.6 collective-permute-start.1
  29.2 0.1 compare_and_fusion.1
  29.3 2.4 collective-permute-start.2
  31.8 0.6 collective-permute-start.3
  32.3 2.4 collective-permute-start.4
  34.7 0.4 broadcast_in_dim.73
  35.2 0.7 collective-permute-start.5
  35.9 10.0 %collective-permute-done.1 = bf16[2,1,512,128]{3,2,1,0:T(8,128)(2,1)S(1)} collective-permute-done((bf16[2,1,512,128]{3,2,1,0:T(8,128)(2,1)}, bf16[2,1,512,128]{3,2,1,0:T(8,128)(2,1)S(1)}, u32[]{:S(2)}, u32[]{:S(2)}) %collective-permute-start.1) | collective-permute-done | bytes 262176 | tf_op jit(solution)/shard_map/ppermute | solution.py:22
  45.8 2.8 %collective-permute-start.6 = (bf16[2,1,512,128]{3,2,1,0:T(8,128)(2,1)S(1)}, bf16[2,1,512,128]{3,2,1,0:T(8,128)(2,1)S(1)}, u32[]{:S(2)}, u32[]{:S(2)}) collective-permute-start(bf16[2,1,512,128]{3,2,1,0:T(8,128)(2,1)S(1)} %get-tuple-element.80), channel_id=1, source_target_pairs={{0,28},{4,24},{8,20},{12,16},{16,12},{20,8},{24,4},{28,0},{1,29},{... | collective-permute-start | bytes 786440 | tf_op jit(solution)/shard_map/ppermute | solution.py:22
  48.7 1.3 collective-permute-done.2
  50.1 14.4 %collective-permute-done.3 = bf16[2,1,512,128]{3,2,1,0:T(8,128)(2,1)S(1)} collective-permute-done((bf16[2,1,512,128]{3,2,1,0:T(8,128)(2,1)}, bf16[2,1,512,128]{3,2,1,0:T(8,128)(2,1)S(1)}, u32[]{:S(2)}, u32[]{:S(2)}) %collective-permute-start.3) | collective-permute-done | bytes 262176 | tf_op jit(solution)/shard_map/ppermute | solution.py:22
  64.6 5.6 %collective-permute-done.4 = bf16[2,1,512,128]{3,2,1,0:T(8,128)(2,1)S(1)} collective-permute-done((bf16[2,1,512,128]{3,2,1,0:T(8,128)(2,1)S(1)}, bf16[2,1,512,128]{3,2,1,0:T(8,128)(2,1)S(1)}, u32[]{:S(2)}, u32[]{:S(2)}) %collective-permute-start.4) | collective-permute-done | bytes 262176 | tf_op jit(solution)/shard_map/ppermute | solution.py:22
  70.3 0.2 pad_maximum_fusion
  70.5 2.9 %gather_fusion.1 = bf16[14,2,512,128]{3,2,1,0:T(8,128)(2,1)} fusion(bf16[2,10,512,128]{3,2,1,0:T(8,128)(2,1)S(1)} %pad_maximum_fusion, s32[1024]{0:T(1024)S(1)} %pad_clamp_fusion), kind=kCustom, calls=%fused_computation.1 | custom fusion | bytes 7340088 | tf_op jit(solution)/shard_map/jit(_take)/gather | solution.py:97
  73.4 2.4 fusion.23
  75.8 2.3 slice_bitcast_fusion
  78.1 83.5 %while.10 = (s32[]{:T(128)}, bf16[2,512,4,128]{3,2,1,0:T(4,128)(2,1)S(1)}, bf16[2,7,512,128]{3,2,1,0:T(8,128)(2,1)}, pred[2,7]{1,0:T(4,128)(4,1)S(1)}, bf16[2,7,...) while((s32[]{:T(128)}, bf16[2,512,4,128]{3,2,1,0:T(4,128)(2,1)S(1)}, ...), condition=%wide.region_4.5_spmd, body=%wide.region_1.4_spmd.sunk | while | flops 3843289088 | bytes 109355664 | solution.py:99
  78.2 1.1 or_and_fusion.2
  79.3 0.2 constant_dynamic-slice_fusion.2
  79.5 13.3 %fusion.38 = (f32[4,512]{1,0:T(4,128)S(1)}, f32[7,512,512,4]{2,1,3,0:T(8,128)}) fusion(pred[512,7,512]{0,2,1:T(8,128)(4,1)S(1)} %or_and_fusion.2, bf16[1,512,4,128]{3,2,1,0:T(4,128)(2,1)S(1)} %constant_dynamic-slice_fusion.2, bf16[2,7,512,128]{3,2,1,0:T(8,128)(2,1)} %get-tuple-element.147, s32[]{:T(128)} %get-tuple-element.136), kind=kOutput, calls=%fused_computation.6.clone.1 | convolution fusion | flops 1901066240 | bytes 32645632 | tf_op jit(solution)/shard_map/while/body/eval_jaxpr/qgd,skd->gqsk/dot_general | solution.py:37
  92.8 12.9 %fusion.39 = f32[4,512]{1,0:T(4,128)S(1)} fusion(f32[7,512,512,4]{2,1,3,0:T(8,128)} %get-tuple-element.127, f32[4,512]{1,0:T(4,128)S(1)} %get-tuple-element.128, pred[512,7,512]{0,2,1:T(8,128)(4,1)S(1)} %or_and_fusion.2), kind=kLoop, calls=%fused_computation.4.clone.1 | loop fusion | flops 29358080 | bytes 31211520 | tf_op jit(solution)/shard_map/while/body/eval_jaxpr/reduce_sum | solution.py:48
  105.7 13.5 %fusion.40 = bf16[1,512,4,128]{1,3,2,0:T(8,128)(2,1)S(1)} fusion(f32[7,512,512,4]{2,1,3,0:T(8,128)} %get-tuple-element.127, f32[4,512]{1,0:T(4,128)S(1)} %get-tuple-element.128, pred[512,7,512]{0,2,1:T(8,128)(4,1)S(1)} %or_and_fusion.2, bf16[2,7,512,128]{3,2,1,0:T(8,128)(2,1)S(1)} %copy-done.1, s32[]{:T(128)} %get-tuple-element.136, ...), kind=kOutput, calls=%fused_computation.13.clone.1 | convolution fusion | flops 1908932608 | bytes 32653316 | tf_op jit(solution)/shard_map/while/body/eval_jaxpr/gqsk,skd->qgd/dot_general | solution.py:49
  119.3 0.3 copy.68
  119.6 0.2 constant_dynamic-update-slice_fusion.9
  120.0 1.1 or_and_fusion.2
  121.0 0.2 constant_dynamic-slice_fusion.2
  121.2 13.3 %fusion.38 = (f32[4,512]{1,0:T(4,128)S(1)}, f32[7,512,512,4]{2,1,3,0:T(8,128)}) fusion(pred[512,7,512]{0,2,1:T(8,128)(4,1)S(1)} %or_and_fusion.2, bf16[1,512,4,128]{3,2,1,0:T(4,128)(2,1)S(1)} %constant_dynamic-slice_fusion.2, bf16[2,7,512,128]{3,2,1,0:T(8,128)(2,1)} %get-tuple-element.147, s32[]{:T(128)} %get-tuple-element.136), kind=kOutput, calls=%fused_computation.6.clone.1 | convolution fusion | flops 1901066240 | bytes 32645632 | tf_op jit(solution)/shard_map/while/body/eval_jaxpr/qgd,skd->gqsk/dot_general | solution.py:37
  134.6 12.9 %fusion.39 = f32[4,512]{1,0:T(4,128)S(1)} fusion(f32[7,512,512,4]{2,1,3,0:T(8,128)} %get-tuple-element.127, f32[4,512]{1,0:T(4,128)S(1)} %get-tuple-element.128, pred[512,7,512]{0,2,1:T(8,128)(4,1)S(1)} %or_and_fusion.2), kind=kLoop, calls=%fused_computation.4.clone.1 | loop fusion | flops 29358080 | bytes 31211520 | tf_op jit(solution)/shard_map/while/body/eval_jaxpr/reduce_sum | solution.py:48
  147.5 13.5 %fusion.40 = bf16[1,512,4,128]{1,3,2,0:T(8,128)(2,1)S(1)} fusion(f32[7,512,512,4]{2,1,3,0:T(8,128)} %get-tuple-element.127, f32[4,512]{1,0:T(4,128)S(1)} %get-tuple-element.128, pred[512,7,512]{0,2,1:T(8,128)(4,1)S(1)} %or_and_fusion.2, bf16[2,7,512,128]{3,2,1,0:T(8,128)(2,1)S(1)} %copy-done.1, s32[]{:T(128)} %get-tuple-element.136, ...), kind=kOutput, calls=%fused_computation.13.clone.1 | convolution fusion | flops 1908932608 | bytes 32653316 | tf_op jit(solution)/shard_map/while/body/eval_jaxpr/gqsk,skd->qgd/dot_general | solution.py:49
  161.0 0.3 copy.68
  161.3 0.2 constant_dynamic-update-slice_fusion.9
  161.6 8.9 %convolution_convert_fusion = bf16[1024,4096]{1,0:T(8,128)(2,1)} fusion(bf16[512,4096]{1,0:T(8,128)(2,1)} %param.11, bf16[128,8,4,128]{3,2,1,0:T(4,128)(2,1)S(1)} %bitcast.127), kind=kOutput, calls=%fused_computation.28 | convolution fusion | flops 4299161600 | bytes 13631488 | tf_op jit(solution)/shard_map/dot_general | solution.py:106
  170.5 77.5 %reduce-scatter.2.cloned.1.call-done = bf16[256,4096]{1,0:T(8,128)(2,1)} async-done(((bf16[1024,4096]{1,0:T(8,128)(2,1)}), bf16[256,4096]{1,0:T(8,128)(2,1)}) %reduce-scatter.2.cloned.1.call-update) | async-done | bytes 2097168 | tf_op jit(solution)/shard_map/reduce_scatter | solution.py:108
  (44 shorter events, 0.7 us)
Async XLA Ops:
  9.0 13.7 %all-to-all-start = ((s32[8,1,1]{2,1,0:T(1,128)}), s32[8,1,1]{2,1,0:T(1,128)S(1)}, u32[]{:S(2)}, u32[]{:S(2)}) async-start(s32[8,1,1]{2,1,0:T(1,128)} %copy.36), calls=%async_computation | async-start | bytes 8192 | tf_op jit(solution)/shard_map/all_to_all | solution.py:80
  16.4 231.7 %reduce-scatter.2.cloned.1.call-start = ((), (), s32[]{:S(2)}) async-start(), calls=%async_computation.2 | async-start | bytes 10485760 | tf_op jit(solution)/shard_map/reduce_scatter | solution.py:108
  27.0 2.2 copy-start.4
  28.1 7.1 %collective-permute-start = (bf16[2,1,512,128]{3,2,1,0:T(8,128)(2,1)}, bf16[2,1,512,128]{3,2,1,0:T(8,128)(2,1)S(1)}, u32[]{:S(2)}, u32[]{:S(2)}) collective-permute-start(bf16[2,1,512,128]{3,2,1,0:T(8,128)(2,1)} %get-tuple-element.86), channel_id=1, source_target_pairs={{0,4},{4,0},{8,12},{12,8},{16,20},{20,16},{24,28},{28,24},{1,5},{5... | collective-permute-start | bytes 786440 | tf_op jit(solution)/shard_map/ppermute | solution.py:22
  28.6 17.2 %collective-permute-start.1 = (bf16[2,1,512,128]{3,2,1,0:T(8,128)(2,1)}, bf16[2,1,512,128]{3,2,1,0:T(8,128)(2,1)S(1)}, u32[]{:S(2)}, u32[]{:S(2)}) collective-permute-start(bf16[2,1,512,128]{3,2,1,0:T(8,128)(2,1)} %get-tuple-element.85), channel_id=1, source_target_pairs={{0,8},{4,12},{8,0},{12,4},{16,24},{20,28},{24,16},{28,20},{1,9},{5... | collective-permute-start | bytes 786440 | tf_op jit(solution)/shard_map/ppermute | solution.py:22
  29.3 20.7 %collective-permute-start.2 = (bf16[2,1,512,128]{3,2,1,0:T(8,128)(2,1)}, bf16[2,1,512,128]{3,2,1,0:T(8,128)(2,1)S(1)}, u32[]{:S(2)}, u32[]{:S(2)}) collective-permute-start(bf16[2,1,512,128]{3,2,1,0:T(8,128)(2,1)} %get-tuple-element.84), channel_id=1, source_target_pairs={{0,12},{4,8},{8,4},{12,0},{16,28},{20,24},{24,20},{28,16},{1,13},{... | collective-permute-start | bytes 786440 | tf_op jit(solution)/shard_map/ppermute | solution.py:22
  31.8 32.8 %collective-permute-start.3 = (bf16[2,1,512,128]{3,2,1,0:T(8,128)(2,1)}, bf16[2,1,512,128]{3,2,1,0:T(8,128)(2,1)S(1)}, u32[]{:S(2)}, u32[]{:S(2)}) collective-permute-start(bf16[2,1,512,128]{3,2,1,0:T(8,128)(2,1)} %get-tuple-element.83), channel_id=1, source_target_pairs={{0,16},{4,20},{8,24},{12,28},{16,0},{20,4},{24,8},{28,12},{1,17},{... | collective-permute-start | bytes 786440 | tf_op jit(solution)/shard_map/ppermute | solution.py:22
  32.3 37.8 %collective-permute-start.4 = (bf16[2,1,512,128]{3,2,1,0:T(8,128)(2,1)S(1)}, bf16[2,1,512,128]{3,2,1,0:T(8,128)(2,1)S(1)}, u32[]{:S(2)}, u32[]{:S(2)}) collective-permute-start(bf16[2,1,512,128]{3,2,1,0:T(8,128)(2,1)S(1)} %get-tuple-element.82), channel_id=1, source_target_pairs={{0,20},{4,16},{8,28},{12,24},{16,4},{20,0},{24,12},{28,8},{1,21},{... | collective-permute-start | bytes 786440 | tf_op jit(solution)/shard_map/ppermute | solution.py:22
  35.1 35.2 %copy-start.2 = (bf16[1024,1,128]{2,0,1:T(8,128)(2,1)S(1)}, bf16[1024,1,128]{2,0,1:T(8,128)(2,1)}, u32[]{:S(2)}) copy-start(bf16[1024,1,128]{2,0,1:T(8,128)(2,1)} %param.9) | copy-start | bytes 786436
  35.1 35.2 %copy-start.3 = (bf16[1024,1,128]{2,0,1:T(8,128)(2,1)S(1)}, bf16[1024,1,128]{2,0,1:T(8,128)(2,1)}, u32[]{:S(2)}) copy-start(bf16[1024,1,128]{2,0,1:T(8,128)(2,1)} %param.8) | copy-start | bytes 786436
  35.2 35.0 %collective-permute-start.5 = (bf16[2,1,512,128]{3,2,1,0:T(8,128)(2,1)S(1)}, bf16[2,1,512,128]{3,2,1,0:T(8,128)(2,1)S(1)}, u32[]{:S(2)}, u32[]{:S(2)}) collective-permute-start(bf16[2,1,512,128]{3,2,1,0:T(8,128)(2,1)S(1)} %get-tuple-element.81), channel_id=1, source_target_pairs={{0,24},{4,28},{8,16},{12,20},{16,8},{20,12},{24,0},{28,4},{1,25},{... | collective-permute-start | bytes 786440 | tf_op jit(solution)/shard_map/ppermute | solution.py:22
  45.8 24.4 %collective-permute-start.6 = (bf16[2,1,512,128]{3,2,1,0:T(8,128)(2,1)S(1)}, bf16[2,1,512,128]{3,2,1,0:T(8,128)(2,1)S(1)}, u32[]{:S(2)}, u32[]{:S(2)}) collective-permute-start(bf16[2,1,512,128]{3,2,1,0:T(8,128)(2,1)S(1)} %get-tuple-element.80), channel_id=1, source_target_pairs={{0,28},{4,24},{8,20},{12,16},{16,12},{20,8},{24,4},{28,0},{1,29},{... | collective-permute-start | bytes 786440 | tf_op jit(solution)/shard_map/ppermute | solution.py:22
  75.8 2.3 copy-start
  75.8 2.3 copy-start.5
  92.8 12.9 %copy-start.1 = (bf16[2,7,512,128]{3,2,1,0:T(8,128)(2,1)S(1)}, bf16[2,7,512,128]{3,2,1,0:T(8,128)(2,1)}, u32[]{:S(2)}) copy-start(bf16[2,7,512,128]{3,2,1,0:T(8,128)(2,1)} %get-tuple-element.145) | copy-start | bytes 5505028 | tf_op jit(solution)/shard_map/while
  134.6 12.9 %copy-start.1 = (bf16[2,7,512,128]{3,2,1,0:T(8,128)(2,1)S(1)}, bf16[2,7,512,128]{3,2,1,0:T(8,128)(2,1)}, u32[]{:S(2)}) copy-start(bf16[2,7,512,128]{3,2,1,0:T(8,128)(2,1)} %get-tuple-element.145) | copy-start | bytes 5505028 | tf_op jit(solution)/shard_map/while
Sparse Core Ops, SparseCore 0:
  170.6 77.3 reduce-scatter.1
